TPU v7x, 256 devices: a whole 4x4x8 slice. The times are simulated.
256 devices in a mesh: member: 2 (over y_hi), seq: 32 (over z, x), head: 4 (over y_lo, core).
Axes of the slice: x: 4, y: 4 (y_hi: 2, y_lo: 2; y = y_hi * 2 + y_lo), z: 8, core: 2. Of those that a mesh axis runs over, the one named last changes fastest.
Arguments:
- tokens: bfloat16 [16384, 5120], P(('seq', 'head')), may hold values from -24 to 24
- lattice: int32 [3, 16384], P(None, 'seq'), may hold values from 0 to 63
- timestep: int32 [32], replicated, may hold values from 0 to 999
- time_weight: bfloat16 [2, 256, 5120], P(None, None, 'seq'), may hold values from -0.375 to 0.375
- query_weight: bfloat16 [2, 5120, 2560], P('member', 'seq', 'head'), may hold values from -6 to 6
- key_weight: bfloat16 [5120, 2560], P('seq', 'head'), may hold values from -6 to 6
- values: bfloat16 [16384, 2560], P(('seq', 'head')), may hold values from -6 to 6
- cotangent: bfloat16 [2, 16384, 2560], P('member', ('seq', 'head')), may hold values from -72 to 72
Outputs:
- fisher: float32 [2, 5120, 2560], P('member', 'seq', 'head')
- merged: float32 [5120, 2560], P('seq', 'head')
All inputs are finite; a program needn't handle non-finite values.
Results may differ from a plain program's by a relative error of at most 0.022.
Values may be sent and summed in bfloat16 or wider, within the bound.
A program may use at most 128 MiB of HBM per device.

v0:
```python
import math
import jax
import jax.numpy as jnp
from jax import lax
from jax.sharding import Mesh
from jax.sharding import PartitionSpec as P

HEAD_SIZE = 128
SEQ = ("seq_0", "seq_1")
SEQ_HEAD = ("seq_0", "seq_1", "head")
damping = 0.01


def side_by_side(arrays, axis, dim, along):
    widths = [a.shape[along] for a in arrays]
    both = jnp.concatenate(arrays, axis=along)
    out = lax.all_gather(both, axis, axis=dim, tiled=True)
    return tuple(jnp.split(out, [sum(widths[:k]) for k in range(1, len(widths))], axis=along))


def own_rows(terms, axes):
    subtotal = terms.astype(jnp.bfloat16)
    for axis in axes:
        subtotal = lax.psum_scatter(subtotal, axis, scatter_dimension=0, tiled=True)
    return subtotal.astype(jnp.float32)


def copy_for_each(array, axis):
    size = lax.axis_size(axis)
    return lax.all_to_all(
        jnp.broadcast_to(array[None], (size, *array.shape)), axis, 0, 0, tiled=True
    )


def of_everyone(array, axis):
    everything = copy_for_each(array, axis)
    return jnp.sum(everything.astype(jnp.float32), axis=0)


def time_features(timestep, feature_count):
    halfway = feature_count // 2
    ladder = jnp.arange(halfway).astype(jnp.float32)
    frequency = jnp.exp(-math.log(10000.0) * 2.0 * ladder / feature_count)
    angles = timestep.astype(jnp.float32)[:, None] * frequency[None, :]
    return jnp.concatenate([jnp.cos(angles), jnp.sin(angles)], axis=1).astype(jnp.bfloat16)


def rope_tables(lattice, head_width):
    halfway = head_width // 2
    side_pairs = head_width // 6
    frame_pairs = halfway - 2 * side_pairs
    column = jnp.arange(head_width)
    pair_index = column % halfway
    which_axis = jnp.where(
        pair_index < frame_pairs, 0, jnp.where(pair_index < frame_pairs + side_pairs, 1, 2)
    )
    anchor = jnp.where(
        which_axis == 0, 0, jnp.where(which_axis == 1, frame_pairs, frame_pairs + side_pairs)
    )
    pair_span = jnp.where(which_axis == 0, frame_pairs, side_pairs)
    frequency = jnp.exp(
        -math.log(10000.0)
        * (pair_index - anchor).astype(jnp.float32)
        / pair_span.astype(jnp.float32)
    )
    position = lattice.astype(jnp.float32)
    angles = jnp.zeros((lattice.shape[1], head_width), jnp.float32)
    for axis_number in range(3):
        chosen = jnp.where(which_axis == axis_number, frequency, 0.0)
        angles = angles + position[axis_number][:, None] * chosen[None, :]
    sign_flip = jnp.where(column < halfway, -1.0, 1.0).astype(jnp.float32)
    return (jnp.cos(angles), jnp.sin(angles) * sign_flip[None, :])


def normed_rotation(stacked, cosine, sine_table):
    halfway = stacked.shape[2] // 2
    inverse = lax.rsqrt(jnp.mean(stacked * stacked, axis=2, keepdims=True) + 1e-06)
    normed = stacked * inverse
    rotated = (
        normed * cosine[:, None, :] + jnp.roll(normed, halfway, axis=2) * sine_table[:, None, :]
    )
    return (normed, inverse, rotated)


def attention_backward(query_pre, key_pre, values, cotangent, cosine, sine_table, head_width):
    length, width = query_pre.shape
    head_count = width // head_width
    halfway = head_width // 2
    query_normed, query_inverse, query_rotated = normed_rotation(
        query_pre.reshape(length, head_count, head_width), cosine, sine_table
    )
    unused_normed, unused_inverse, key_rotated = normed_rotation(
        key_pre.reshape(length, head_count, head_width), cosine, sine_table
    )
    query_round = query_rotated.astype(jnp.bfloat16)
    key_round = key_rotated.astype(jnp.bfloat16)
    value_heads = values.reshape(length, head_count, head_width)
    block_rows = min(length, 512)
    block_count = length // block_rows
    score_scale = head_width ** (-0.5)

    def one_block(portion):
        query_block, grad_block = portion
        scores = (
            jnp.einsum("qhd,khd->hqk", query_block, key_round, preferred_element_type=jnp.float32)
            * score_scale
        )
        raised = jnp.exp(scores)
        weights = raised / jnp.sum(raised, axis=2, keepdims=True)
        rounded = weights.astype(jnp.bfloat16)
        attended = jnp.einsum(
            "hqk,khd->qhd", rounded, value_heads, preferred_element_type=jnp.float32
        )
        inner = jnp.sum(grad_block.astype(jnp.float32) * attended, axis=2)
        grad_weights = jnp.einsum(
            "qhd,khd->hqk", grad_block, value_heads, preferred_element_type=jnp.float32
        )
        grad_scores = (weights * (grad_weights - inner.T[:, :, None])).astype(jnp.bfloat16)
        return (
            jnp.einsum("hqk,khd->qhd", grad_scores, key_round, preferred_element_type=jnp.float32)
            * score_scale
        )

    grad_rotated = lax.map(
        one_block,
        (
            query_round.reshape(block_count, block_rows, head_count, head_width),
            cotangent.reshape(block_count, block_rows, head_count, head_width),
        ),
    )
    grad_rotated = grad_rotated.reshape(length, head_count, head_width)
    grad_normed = grad_rotated * cosine[:, None, :] + jnp.roll(
        grad_rotated * sine_table[:, None, :], halfway, axis=2
    )
    grad_query = query_inverse * (
        grad_normed - query_normed * jnp.mean(grad_normed * query_normed, axis=2, keepdims=True)
    )
    return grad_query.reshape(length, width).astype(jnp.bfloat16)


def on_device(tokens, lattice, timestep, time_weight, query_weight, key_weight, values, cotangent):
    features = time_features(timestep, time_weight.shape[1])
    local_shift = jnp.einsum(
        "cf,jfd->cjd", features, time_weight, preferred_element_type=jnp.float32
    )
    own_shift = lax.all_to_all(
        local_shift.astype(jnp.bfloat16), SEQ, split_axis=0, concat_axis=2, tiled=True
    ).astype(local_shift.dtype)
    hidden = tokens.astype(jnp.float32)
    average = jnp.mean(hidden, axis=1, keepdims=True)
    centred = hidden - average
    variance = jnp.mean(centred * centred, axis=1, keepdims=True)
    normed = centred * lax.rsqrt(variance + 1e-06)
    modulated = (normed * (1.0 + own_shift[0, 1][None, :]) + own_shift[0, 0][None, :]).astype(
        jnp.bfloat16
    )
    clip_rows = lax.all_gather(modulated, "head", axis=0, tiled=True)
    cosine, sine_table = rope_tables(lattice, HEAD_SIZE)
    own_query = query_weight[0]

    def contract(portion):
        return jnp.dot(clip_rows, portion, preferred_element_type=jnp.float32)

    portions = side_by_side((own_query, key_weight), SEQ, 0, 1)
    query_pre = contract(portions[0])
    key_pre = contract(portions[1])
    value_heads, cot_heads = (
        lax.all_to_all(values, "head", split_axis=1, concat_axis=0, tiled=True),
        lax.all_to_all(cotangent[0], "head", split_axis=1, concat_axis=0, tiled=True),
    )
    grad_query = attention_backward(
        query_pre, key_pre, value_heads, cot_heads, cosine, sine_table, HEAD_SIZE
    )
    grad = lax.dot_general(
        clip_rows, grad_query, (((0,), (0,)), ((), ())), preferred_element_type=jnp.float32
    )
    fisher = own_rows(grad * grad, SEQ)
    weighted = fisher + damping
    upper = weighted * own_query.astype(jnp.float32)
    upper_sum, lower_sum = (
        of_everyone(upper.astype(jnp.bfloat16), "member").astype(jnp.float32),
        of_everyone(weighted.astype(jnp.bfloat16), "member").astype(jnp.float32),
    )
    merged = upper_sum / lower_sum
    return (fisher[None], merged)


def solution(mesh):
    finer = Mesh(
        mesh.devices.reshape(mesh.shape["member"], 8, 4, mesh.shape["head"]),
        ("member", "seq_0", "seq_1", "head"),
    )
    in_specs = (
        P(SEQ_HEAD, None),
        P(None, SEQ),
        P(),
        P(None, None, SEQ),
        P("member", SEQ, "head"),
        P(SEQ, "head"),
        P(SEQ_HEAD, None),
        P("member", SEQ_HEAD, None),
    )
    out_specs = (P("member", SEQ, "head"), P(SEQ, "head"))
    return jax.shard_map(
        on_device, mesh=finer, in_specs=in_specs, out_specs=out_specs, check_vma=False
    )
```

profile of v0, /device:TPU:32, one launch (start us, length us, event | category | flops | bytes accessed | tf_op | source)
XLA Modules:
  0.0 387.7 jit_solution(6202035833007734098)
XLA Ops:
  7.2 0.8 convert_element_type.123
  8.1 0.1 convolution_convert_fusion
  8.3 0.7 copy.51
  8.9 11.2 %all-to-all-start = ((bf16[32,2,160]{2,1,0:T(2,128)(2,1)}), bf16[32,2,160]{2,1,0:T(2,128)(2,1)S(1)}, u32[]{:S(2)}, u32[]{:S(2)}) async-start(bf16[32,2,160]{2,1,0:T(2,128)(2,1)} %copy.51), calls=%async_computation | async-start | bytes 65536 | tf_op jit(solution)/shard_map/all_to_all | solution.py:146
  20.2 1.6 convert_reduce_fusion
  21.8 0.5 fusion.8
  22.3 6.5 %all-to-all-done = bf16[32,2,160]{2,1,0:T(2,128)(2,1)S(1)} async-done(((bf16[32,2,160]{2,1,0:T(2,128)(2,1)}), bf16[32,2,160]{2,1,0:T(2,128)(2,1)S(1)}, u32[]{:S(2)}, u32[]{:S(2)}) %all-to-all-start) | async-done | bytes 20512 | tf_op jit(solution)/shard_map/all_to_all | solution.py:146
  29.0 1.7 fusion.11
  30.8 0.9 copy-done.6
  31.7 0.8 pad_maximum_fusion
  32.5 1.1 copy.59
  33.6 3.5 all-to-all-start.2
  37.2 1.1 copy.57
  38.2 14.3 %all-to-all-done.2 = bf16[128,4,640]{0,2,1:T(8,128)(2,1)S(1)} async-done(((bf16[128,4,640]{0,2,1:T(8,128)(2,1)}), bf16[128,4,640]{0,2,1:T(8,128)(2,1)S(1)}, u32[]{:S(2)}, u32[]{:S(2)}) %all-to-all-start.2) | async-done | bytes 655392 | tf_op jit(solution)/shard_map/all_to_all | solution.py:168
  52.5 3.5 all-to-all-start.1
  56.1 2.0 broadcast_multiply_fusion.3
  58.1 0.5 copy.60
  58.6 1.1 reshape.305
  59.8 13.9 %all-to-all-done.1 = bf16[128,4,640]{0,2,1:T(8,128)(2,1)S(1)} async-done(((bf16[128,4,640]{0,2,1:T(8,128)(2,1)}), bf16[128,4,640]{0,2,1:T(8,128)(2,1)S(1)}, u32[]{:S(2)}, u32[]{:S(2)}) %all-to-all-start.1) | async-done | bytes 655392 | tf_op jit(solution)/shard_map/all_to_all | solution.py:169
  73.6 0.5 copy.58
  74.2 1.1 squeeze.12
  75.2 21.1 %all-gather.3.cloned.1.call-done = bf16[512,5120]{1,0:T(8,128)(2,1)} async-done(((bf16[128,5120]{1,0:T(8,128)(2,1)}), bf16[512,5120]{1,0:T(8,128)(2,1)}) %all-gather.3.cloned.1.call-update) | async-done | bytes 5242896 | tf_op jit(solution)/shard_map/all_gather | solution.py:157
  96.3 118.9 %all-gather.5.cloned.1.call-done = bf16[5120,1280]{1,0:T(8,128)(2,1)} async-done(((bf16[160,1280]{1,0:T(8,128)(2,1)}), bf16[5120,1280]{1,0:T(8,128)(2,1)}) %all-gather.5.cloned.1.call-update) | async-done | bytes 13107216 | tf_op jit(solution)/shard_map/all_gather | solution.py:17
  215.2 8.4 %fusion = f32[512,640]{0,1:T(8,128)S(1)} fusion(bf16[512,5120]{1,0:T(8,128)(2,1)} %all-gather.3.cloned.1.call-done, bf16[5120,1280]{1,0:T(8,128)(2,1)} %all-gather.5.cloned.1.call-done), kind=kOutput, calls=%fused_computation.1 | convolution fusion | flops 3355443200 | bytes 13107200 | tf_op jit(solution)/shard_map/dot_general | solution.py:162
  223.6 0.2 multiply_reduce_fusion.1
  224.0 2.2 copy-done.15
  226.3 6.0 %fusion.2 = f32[512,640]{0,1:T(8,128)S(1)} fusion(bf16[512,5120]{1,0:T(8,128)(2,1)S(1)} %copy-done.15, bf16[5120,1280]{1,0:T(8,128)(2,1)} %all-gather.5.cloned.1.call-done), kind=kOutput, calls=%fused_computation.3 | convolution fusion | flops 3355443200 | bytes 13107200 | tf_op jit(solution)/shard_map/dot_general | solution.py:162
  232.2 0.2 multiply_reduce_fusion.2
  232.7 0.8 copy-done.4
  233.6 0.4 fusion.28
  234.0 1.2 fusion.5
  235.3 1.2 fusion.31
  236.5 1.1 copy-done.2
  237.6 5.9 %broadcast_multiply_fusion = (f32[512,5,128]{0,2,1:T(8,128)}, f32[512,5,128]{0,2,1:T(8,128)S(1)}) fusion(f32[512,128]{0,1:T(8,128)} %get-tuple-element.30, bf16[512,5,128]{0,2,1:T(8,128)(2,1)S(1)} %fusion.28, bf16[512,5,128]{0,2,1:T(8,128)(2,1)} %squeeze.12, bf16[512,5,128]{0,2,1:T(8,128)(2,1)} %reshape.305, f32[5,512]{1,0:T(8,128)S(1)} %bitcast.67, ...), kind=kOutput, calls=%fused_computation.41 | convolution fusion | flops 677969920 | bytes 10113024 | tf_op jit(solution)/shard_map/while/body/eval_jaxpr/hqk,khd->qhd/dot_general | solution.py:120
  243.5 1.6 fusion.53
  245.1 0.5 multiply_reduce_fusion
  245.6 0.6 multiply_convert_fusion.5
  246.2 0.4 slice-done.1
  246.7 6.3 %multiply_convert_fusion = bf16[5120,640]{1,0:T(8,128)(2,1)} fusion(bf16[512,5120]{1,0:T(8,128)(2,1)S(1)} %bitcast.66, bf16[512,640]{0,1:T(8,128)(2,1)S(1)} %bitcast.59), kind=kOutput, calls=%fused_computation | convolution fusion | flops 3361996800 | bytes 12451840 | tf_op jit(solution)/shard_map/dot_general | solution.py:174
  253.0 74.8 %reduce-scatter.3.cloned.1.call-done = bf16[640,640]{1,0:T(8,128)(2,1)} async-done(((bf16[5120,640]{1,0:T(8,128)(2,1)}), bf16[640,640]{1,0:T(8,128)(2,1)}) %reduce-scatter.3.cloned.1.call-update) | async-done | bytes 819216 | tf_op jit(solution)/shard_map/reduce_scatter | solution.py:24
  327.8 27.9 %reduce-scatter.5.cloned.1.call-done = bf16[160,640]{1,0:T(8,128)(2,1)} async-done(((bf16[640,640]{1,0:T(8,128)(2,1)}), bf16[160,640]{1,0:T(8,128)(2,1)}) %reduce-scatter.5.cloned.1.call-update) | async-done | bytes 204816 | tf_op jit(solution)/shard_map/reduce_scatter | solution.py:24
  355.8 1.0 fusion.38
  356.8 11.7 %all_to_all.51 = bf16[2,160,640]{2,1,0:T(8,128)(2,1)S(1)} all-to-all(bf16[2,160,640]{2,1,0:T(8,128)(2,1)S(1)} %broadcast_in_dim.82), channel_id=1, replica_groups=mesh['member'=2,'seq_0'=8,'seq_1'=4,'head'=4] {'member'}, dimensions={0} | all-to-all | bytes 819200 | tf_op jit(solution)/shard_map/all_to_all | solution.py:30
  368.6 0.8 broadcast_in_dim.81
  369.3 3.5 all-to-all-start.3
  372.8 0.8 convert_bitcast_fusion
  373.7 6.6 %all-to-all-done.3 = bf16[2,160,640]{2,1,0:T(8,128)(2,1)S(1)} async-done(((bf16[2,160,640]{2,1,0:T(8,128)(2,1)}), bf16[2,160,640]{2,1,0:T(8,128)(2,1)S(1)}, u32[]{:S(2)}, u32[]{:S(2)}) %all-to-all-start.3) | async-done | bytes 409632 | tf_op jit(solution)/shard_map/all_to_all | solution.py:30
  380.3 0.9 div.63
  (62 shorter events, 1.5 us)
Async XLA Ops:
  7.2 1.0 copy-start
  7.2 14.6 %copy-start.1 = (bf16[128,5120]{1,0:T(8,128)(2,1)S(1)}, bf16[128,5120]{1,0:T(8,128)(2,1)}, u32[]{:S(2)}) copy-start(bf16[128,5120]{1,0:T(8,128)(2,1)} %param.8) | copy-start | bytes 3932164
  8.9 19.9 %all-to-all-start = ((bf16[32,2,160]{2,1,0:T(2,128)(2,1)}), bf16[32,2,160]{2,1,0:T(2,128)(2,1)S(1)}, u32[]{:S(2)}, u32[]{:S(2)}) async-start(bf16[32,2,160]{2,1,0:T(2,128)(2,1)} %copy.51), calls=%async_computation | async-start | bytes 65536 | tf_op jit(solution)/shard_map/all_to_all | solution.py:146
  20.1 76.2 %all-gather.3.cloned.1.call-start = ((), (), s32[]{:S(2)}) async-start(), calls=%async_computation.7 | async-start | bytes 6553600 | tf_op jit(solution)/shard_map/all_gather | solution.py:157
  30.7 0.9 copy-start.6
  30.7 1.0 copy-start.13
  30.7 1.8 copy-start.9
  30.7 184.5 %all-gather.5.cloned.1.call-start = ((), (), s32[]{:S(2)}) async-start(), calls=%async_computation.8 | async-start | bytes 13516800 | tf_op jit(solution)/shard_map/all_gather | solution.py:17
  32.5 4.6 %copy-start.10 = (bf16[1,128,2560]{2,1,0:T(8,128)(2,1)S(1)}, bf16[1,128,2560]{2,1,0:T(8,128)(2,1)}, u32[]{:S(2)}) copy-start(bf16[1,128,2560]{2,1,0:T(8,128)(2,1)} %param.15) | copy-start | bytes 1966084
  33.6 18.9 %all-to-all-start.2 = ((bf16[128,4,640]{0,2,1:T(8,128)(2,1)}), bf16[128,4,640]{0,2,1:T(8,128)(2,1)S(1)}, u32[]{:S(2)}, u32[]{:S(2)}) async-start(bf16[128,4,640]{0,2,1:T(8,128)(2,1)} %bitcast.13), calls=%async_computation.2 | async-start | bytes 1310720 | tf_op jit(solution)/shard_map/all_to_all | solution.py:168
  37.1 18.9 %copy-start.14 = (s32[3,512]{1,0:T(4,128)S(1)}, s32[3,512]{1,0:T(4,128)}, u32[]{:S(2)}) copy-start(s32[3,512]{1,0:T(4,128)} %param.9) | copy-start | bytes 18436
  52.5 21.1 %all-to-all-start.1 = ((bf16[128,4,640]{0,2,1:T(8,128)(2,1)}), bf16[128,4,640]{0,2,1:T(8,128)(2,1)S(1)}, u32[]{:S(2)}, u32[]{:S(2)}) async-start(bf16[128,4,640]{0,2,1:T(8,128)(2,1)} %bitcast.11), calls=%async_computation.1 | async-start | bytes 1310720 | tf_op jit(solution)/shard_map/all_to_all | solution.py:169
  56.0 271.8 %reduce-scatter.3.cloned.1.call-start = ((), (), s32[]{:S(2)}) async-start(), calls=%async_computation.9 | async-start | bytes 7372800 | tf_op jit(solution)/shard_map/reduce_scatter | solution.py:24
  223.8 2.5 copy-start.15
  232.6 1.0 copy-start.4
  232.6 1.0 copy-start.5
  234.0 1.3 copy-start.11
  234.0 1.3 copy-start.12
  235.3 2.3 copy-start.2
  243.5 1.6 copy-start.3
  243.5 2.7 slice-start
  245.1 1.6 slice-start.1
  252.9 102.9 %copy-start.7 = (bf16[1,160,640]{2,1,0:T(8,128)(2,1)S(1)}, bf16[1,160,640]{2,1,0:T(8,128)(2,1)}, u32[]{:S(2)}) copy-start(bf16[1,160,640]{2,1,0:T(8,128)(2,1)} %param.12) | copy-start | bytes 614404
  252.9 102.8 %reduce-scatter.5.cloned.1.call-start = ((), (), s32[]{:S(2)}) async-start(), calls=%async_computation.10 | async-start | bytes 1024000 | tf_op jit(solution)/shard_map/reduce_scatter | solution.py:24
  356.8 16.0 %copy-start.8 = (bf16[160,640]{1,0:T(8,128)(2,1)S(1)}, bf16[160,640]{1,0:T(8,128)(2,1)}, u32[]{:S(2)}) copy-start(bf16[160,640]{1,0:T(8,128)(2,1)} %reduce-scatter.5.cloned.1.call-done) | copy-start | bytes 614404
  369.3 10.9 %all-to-all-start.3 = ((bf16[2,160,640]{2,1,0:T(8,128)(2,1)}), bf16[2,160,640]{2,1,0:T(8,128)(2,1)S(1)}, u32[]{:S(2)}, u32[]{:S(2)}) async-start(bf16[2,160,640]{2,1,0:T(8,128)(2,1)} %broadcast_in_dim.81), calls=%async_computation.5 | async-start | bytes 819200 | tf_op jit(solution)/shard_map/all_to_all | solution.py:30
Sparse Core Ops, SparseCore 0:
  30.8 65.4 all-gather.2
  99.5 115.6 all-gather.4
  253.1 74.6 reduce-scatter.2
  330.2 25.5 reduce-scatter.4
where the time goes:
time: 388 us
  waiting for transfers between devices  284 us (73%)
  matrix products  29.1 us (8%)
  starting transfers between devices  21.8 us (6%)
  local copies, waits for them, and re-layouts  14.4 us (4%)
  between operations  14.2 us (4%)
  other arithmetic  12.4 us (3%)
  blocking collectives  11.7 us (3%)
    all_gather x1, waiting for transfers between devices, side_by_side(): out = lax.all_gather(both, axis, axis=dim, tiled=True)  119 us
    reduce_scatter x2, waiting for transfers between devices, own_rows(): subtotal = lax.psum_scatter(subtotal, axis, scatter_dimension=0, tiled=True)  103 us
    all_gather x1, waiting for transfers between devices, on_device(): clip_rows = lax.all_gather(modulated, 'head', axis=0, tiled=True)  21.1 us
    dot_general x2, matrix products, contract(): return jnp.dot(clip_rows, portion, preferred_element_type=jnp.float32)  14.4 us
    all_to_all x1, waiting for transfers between devices, on_device(): lax.all_to_all(values, 'head', split_axis=1, concat_axis=0, tiled=True)  14.3 us
    all_to_all x1, waiting for transfers between devices, on_device(): lax.all_to_all(cotangent[0], 'head', split_axis=1, concat_axis=0, tiled=T...  13.9 us
    all_to_all x1, blocking collectives, copy_for_each(): lax.all_to_all(jnp.broadcast_to(array[None], (size, *array.shape)), axis,...  11.7 us
    all_to_all x1, starting transfers between devices, on_device(): lax.all_to_all(local_shift.astype(jnp.bfloat16), SEQ, split_axis=0, conca...  11.2 us
  transfers between devices with their start and end apart: 8, of which 8 were waited for; matrix products, arithmetic and copies ran while one was open for 3% of the time, Pallas kernels for 0%

commit v1 on v0

--- a/solution.py
+++ b/solution.py
@@ -154,7 +154,9 @@
     modulated = (normed * (1.0 + own_shift[0, 1][None, :]) + own_shift[0, 0][None, :]).astype(
         jnp.bfloat16
     )
-    clip_rows = lax.all_gather(modulated, "head", axis=0, tiled=True)
+    clip_rows = jnp.concatenate(
+        lax.all_to_all(jnp.stack([modulated] * lax.axis_size("head")), "head", 0, 0), axis=0
+    )
     cosine, sine_table = rope_tables(lattice, HEAD_SIZE)
     own_query = query_weight[0]
 

time: 388 us -> 339 us (0.87)
  waiting for transfers between devices: 284 us -> 195 us
  local copies, waits for them, and re-layouts: 14.4 us -> 46.2 us
  starting transfers between devices: 21.8 us -> 27.7 us
    all_gather x1, waiting for transfers between devices: 119 us -> 59.9 us  [side_by_side(): out = lax.all_gather(both, axis, axis=dim, tiled=True)]
    dot_general x0 -> x3, local copies, waits for them, and re-layouts: none -> 29.6 us  [contract(): return jnp.dot(clip_rows, portion, preferred_element_type=jnp.float32)]
    all_gather x1 -> x0, waiting for transfers between devices: 21.1 us -> none  [on_device(): clip_rows = lax.all_gather(modulated, 'head', axis=0, tiled=True)]
    all_to_all x0 -> x1, starting transfers between devices: none -> 5.21 us  [on_device(): lax.all_to_all(jnp.stack([modulated] * lax.axis_size('head')), 'head', 0, 0)]
    all_to_all x1, waiting for transfers between devices: 14.3 us -> 9.98 us  [on_device(): lax.all_to_all(values, 'head', split_axis=1, concat_axis=0, tiled=True)]
    all_to_all x1, waiting for transfers between devices: 13.9 us -> 9.7 us  [on_device(): lax.all_to_all(cotangent[0], 'head', split_axis=1, concat_axis=0, tiled=T...]
    unnamed x38 -> x34, local copies, waits for them, and re-layouts: 7.86 us -> 4.88 us
  transfers between devices with their start and end apart: 8 -> 8, of which waited for: 8 -> 7; matrix products, arithmetic and copies ran while one was open for 3% -> 11% of each run, Pallas kernels for 0% -> 0%
where the time goes in v1:
time: 339 us; the launch traced here: 338 us
  waiting for transfers between devices  195 us (58%)
  local copies, waits for them, and re-layouts  46.2 us (14%)
  matrix products  32.7 us (10%)
  starting transfers between devices  27.7 us (8%)
  between operations  14.1 us (4%)
  blocking collectives  11.5 us (3%)
  other arithmetic  10.7 us (3%)
    reduce_scatter x2, waiting for transfers between devices, own_rows(): subtotal = lax.psum_scatter(subtotal, axis, scatter_dimension=0, tiled=True)  103 us
    all_gather x1, waiting for transfers between devices, side_by_side(): out = lax.all_gather(both, axis, axis=dim, tiled=True)  59.9 us
    dot_general x3, local copies, waits for them, and re-layouts, contract(): return jnp.dot(clip_rows, portion, preferred_element_type=jnp.float32)  29.6 us
    dot_general x2, matrix products, contract(): return jnp.dot(clip_rows, portion, preferred_element_type=jnp.float32)  14.8 us
    all_to_all x1, blocking collectives, copy_for_each(): lax.all_to_all(jnp.broadcast_to(array[None], (size, *array.shape)), axis,...  11.5 us
    all_to_all x1, starting transfers between devices, on_device(): lax.all_to_all(local_shift.astype(jnp.bfloat16), SEQ, split_axis=0, conca...  11.2 us
    all_to_all x1, waiting for transfers between devices, on_device(): lax.all_to_all(values, 'head', split_axis=1, concat_axis=0, tiled=True)  9.98 us
    all_to_all x1, waiting for transfers between devices, on_device(): lax.all_to_all(cotangent[0], 'head', split_axis=1, concat_axis=0, tiled=T...  9.7 us
  transfers between devices with their start and end apart: 8, of which 7 were waited for; matrix products, arithmetic and copies ran while one was open for 11% of the time, Pallas kernels for 0%

profile of v1, /device:TPU:32, one launch (start us, length us, event | category | flops | bytes accessed | tf_op | source)
XLA Modules:
  0.0 337.8 jit_solution(9999758674598535150)
XLA Ops:
  7.2 1.9 pad_maximum_fusion
  9.2 0.7 convert_element_type.123
  10.2 0.7 copy.51
  10.8 11.2 %all-to-all-start = ((bf16[32,2,160]{2,1,0:T(2,128)(2,1)}), bf16[32,2,160]{2,1,0:T(2,128)(2,1)S(1)}, u32[]{:S(2)}, u32[]{:S(2)}) async-start(bf16[32,2,160]{2,1,0:T(2,128)(2,1)} %copy.51), calls=%async_computation | async-start | bytes 65536 | tf_op jit(solution)/shard_map/all_to_all | solution.py:146
  22.0 0.3 convert_reduce_fusion
  22.3 0.5 fusion.4
  22.8 0.3 copy-done.11
  23.1 1.1 copy.59
  24.2 1.1 copy.57
  25.3 5.5 %all-to-all-done = bf16[32,2,160]{2,1,0:T(2,128)(2,1)S(1)} async-done(((bf16[32,2,160]{2,1,0:T(2,128)(2,1)}), bf16[32,2,160]{2,1,0:T(2,128)(2,1)S(1)}, u32[]{:S(2)}, u32[]{:S(2)}) %all-to-all-start) | async-done | bytes 20512 | tf_op jit(solution)/shard_map/all_to_all | solution.py:146
  30.8 3.5 %all-to-all-start.3 = ((bf16[128,4,640]{0,2,1:T(8,128)(2,1)}), bf16[128,4,640]{0,2,1:T(8,128)(2,1)S(1)}, u32[]{:S(2)}, u32[]{:S(2)}) async-start(bf16[128,4,640]{0,2,1:T(8,128)(2,1)} %bitcast.18), calls=%async_computation.3 | async-start | bytes 1310720 | tf_op jit(solution)/shard_map/all_to_all | solution.py:170
  34.5 10.0 %all-to-all-done.3 = bf16[128,4,640]{0,2,1:T(8,128)(2,1)S(1)} async-done(((bf16[128,4,640]{0,2,1:T(8,128)(2,1)}), bf16[128,4,640]{0,2,1:T(8,128)(2,1)S(1)}, u32[]{:S(2)}, u32[]{:S(2)}) %all-to-all-start.3) | async-done | bytes 655392 | tf_op jit(solution)/shard_map/all_to_all | solution.py:170
  44.5 4.2 %all-to-all-start.2 = ((bf16[128,4,640]{0,2,1:T(8,128)(2,1)}), bf16[128,4,640]{0,2,1:T(8,128)(2,1)}, u32[]{:S(2)}, u32[]{:S(2)}) async-start(bf16[128,4,640]{0,2,1:T(8,128)(2,1)} %bitcast.16), calls=%async_computation.2 | async-start | bytes 1310720 | tf_op jit(solution)/shard_map/all_to_all | solution.py:171
  48.6 0.6 fusion.7
  49.2 9.7 %all-to-all-done.2 = bf16[128,4,640]{0,2,1:T(8,128)(2,1)} async-done(((bf16[128,4,640]{0,2,1:T(8,128)(2,1)}), bf16[128,4,640]{0,2,1:T(8,128)(2,1)}, u32[]{:S(2)}, u32[]{:S(2)}) %all-to-all-start.2) | async-done | bytes 655392 | tf_op jit(solution)/shard_map/all_to_all | solution.py:171
  58.9 3.0 stack.2
  61.9 5.2 %all-to-all-start.1 = ((bf16[4,128,5120]{2,1,0:T(8,128)(2,1)}), bf16[4,128,5120]{2,1,0:T(8,128)(2,1)}, u32[]{:S(2)}, u32[]{:S(2)}) async-start(bf16[4,128,5120]{2,1,0:T(8,128)(2,1)} %stack.2), calls=%async_computation.1 | async-start | bytes 10485760 | tf_op jit(solution)/shard_map/all_to_all | solution.py:158
  67.3 2.0 broadcast_multiply_fusion.3
  69.3 0.5 copy.60
  69.8 1.1 reshape.307
  70.9 1.6 copy.58
  72.5 1.1 squeeze.12
  73.6 59.9 %all-gather.2.cloned.1.call-done = bf16[5120,1280]{1,0:T(8,128)(2,1)} async-done(((bf16[160,1280]{1,0:T(8,128)(2,1)}), bf16[5120,1280]{1,0:T(8,128)(2,1)}) %all-gather.2.cloned.1.call-update) | async-done | bytes 13107216 | tf_op jit(solution)/shard_map/all_gather | solution.py:17
  133.5 10.6 %slice_bitcast_fusion = (bf16[640,5120]{0,1:T(8,128)(2,1)}, bf16[640,5120]{0,1:T(8,128)(2,1)}) fusion(bf16[5120,1280]{1,0:T(8,128)(2,1)} %all-gather.2.cloned.1.call-done), kind=kLoop, calls=%fused_computation.1 | loop fusion | bytes 26214400 | tf_op jit(solution)/shard_map/dot_general | solution.py:164
  144.1 9.5 %copy.54 = bf16[640,5120]{1,0:T(8,128)(2,1)} copy(bf16[640,5120]{0,1:T(8,128)(2,1)} %get-tuple-element.14) | data formatting | bytes 13107200 | tf_op jit(solution)/shard_map/dot_general | solution.py:164
  153.6 7.3 %multiply_reduce_fusion.1 = (f32[512,5]{0,1:T(8,128)S(1)}, f32[512,5,128]{0,2,1:T(8,128)S(1)}) fusion(bf16[512,5120,1]{1,0,2:T(8,128)(2,1)} %bitcast.6, bf16[5,128,5120]{2,1,0:T(8,128)(2,1)} %bitcast.58), kind=kOutput, calls=%fused_computation.32 | convolution fusion | flops 3356096000 | bytes 13117440 | tf_op jit(solution)/shard_map/dot_general | solution.py:164
  161.1 1.2 fusion.51
  162.4 9.5 %copy.53 = bf16[640,5120]{1,0:T(8,128)(2,1)} copy(bf16[640,5120]{0,1:T(8,128)(2,1)} %get-tuple-element.15) | data formatting | bytes 13107200 | tf_op jit(solution)/shard_map/dot_general | solution.py:164
  171.9 7.5 %multiply_reduce_fusion.2 = (f32[512,5]{0,1:T(8,128)S(1)}, f32[512,5,128]{0,2,1:T(8,128)S(1)}) fusion(bf16[512,5120,1]{1,0,2:T(8,128)(2,1)} %bitcast.6, bf16[5,128,5120]{2,1,0:T(8,128)(2,1)} %bitcast.59), kind=kOutput, calls=%fused_computation.33 | convolution fusion | flops 3356096000 | bytes 13117440 | tf_op jit(solution)/shard_map/dot_general | solution.py:164
  179.7 0.9 copy-done.4
  181.0 0.4 fusion.24
  181.4 1.1 fusion.1
  182.7 1.2 fusion.27
  183.9 1.0 copy-done.3
  184.8 5.9 %broadcast_multiply_fusion = (f32[512,5,128]{0,2,1:T(8,128)}, f32[512,5,128]{0,2,1:T(8,128)S(1)}) fusion(f32[512,128]{0,1:T(8,128)} %get-tuple-element.32, bf16[512,5,128]{0,2,1:T(8,128)(2,1)S(1)} %fusion.24, bf16[512,5,128]{0,2,1:T(8,128)(2,1)} %squeeze.12, bf16[512,5,128]{0,2,1:T(8,128)(2,1)} %reshape.307, f32[5,512]{1,0:T(8,128)S(1)} %bitcast.68, ...), kind=kOutput, calls=%fused_computation.39 | convolution fusion | flops 677969920 | bytes 10113024 | tf_op jit(solution)/shard_map/while/body/eval_jaxpr/hqk,khd->qhd/dot_general | solution.py:120
  190.8 1.5 fusion.49
  192.2 0.5 multiply_reduce_fusion
  192.8 0.6 multiply_convert_fusion.5
  193.4 9.5 %multiply_convert_fusion = bf16[5120,640]{1,0:T(8,128)(2,1)} fusion(bf16[512,5120]{1,0:T(8,128)(2,1)} %bitcast.5, bf16[512,640]{0,1:T(8,128)(2,1)S(1)} %bitcast.62), kind=kOutput, calls=%fused_computation | convolution fusion | flops 3361996800 | bytes 12451840 | tf_op jit(solution)/shard_map/dot_general | solution.py:176
  203.0 74.8 %reduce-scatter.3.cloned.1.call-done = bf16[640,640]{1,0:T(8,128)(2,1)} async-done(((bf16[5120,640]{1,0:T(8,128)(2,1)}), bf16[640,640]{1,0:T(8,128)(2,1)}) %reduce-scatter.3.cloned.1.call-update) | async-done | bytes 819216 | tf_op jit(solution)/shard_map/reduce_scatter | solution.py:24
  277.8 28.3 %reduce-scatter.5.cloned.1.call-done = bf16[160,640]{1,0:T(8,128)(2,1)} async-done(((bf16[640,640]{1,0:T(8,128)(2,1)}), bf16[160,640]{1,0:T(8,128)(2,1)}) %reduce-scatter.5.cloned.1.call-update) | async-done | bytes 204816 | tf_op jit(solution)/shard_map/reduce_scatter | solution.py:24
  306.1 1.0 fusion.34
  307.2 11.5 %all_to_all.56 = bf16[2,160,640]{2,1,0:T(8,128)(2,1)S(1)} all-to-all(bf16[2,160,640]{2,1,0:T(8,128)(2,1)S(1)} %broadcast_in_dim.82), channel_id=1, replica_groups=mesh['member'=2,'seq_0'=8,'seq_1'=4,'head'=4] {'member'}, dimensions={0} | all-to-all | bytes 819200 | tf_op jit(solution)/shard_map/all_to_all | solution.py:30
  318.7 0.8 broadcast_in_dim.81
  319.5 3.5 %all-to-all-start.4 = ((bf16[2,160,640]{2,1,0:T(8,128)(2,1)}), bf16[2,160,640]{2,1,0:T(8,128)(2,1)S(1)}, u32[]{:S(2)}, u32[]{:S(2)}) async-start(bf16[2,160,640]{2,1,0:T(8,128)(2,1)} %broadcast_in_dim.81), calls=%async_computation.6 | async-start | bytes 819200 | tf_op jit(solution)/shard_map/all_to_all | solution.py:30
  323.0 0.8 convert_bitcast_fusion
  323.8 6.6 %all-to-all-done.4 = bf16[2,160,640]{2,1,0:T(8,128)(2,1)S(1)} async-done(((bf16[2,160,640]{2,1,0:T(8,128)(2,1)}), bf16[2,160,640]{2,1,0:T(8,128)(2,1)S(1)}, u32[]{:S(2)}, u32[]{:S(2)}) %all-to-all-start.4) | async-done | bytes 409632 | tf_op jit(solution)/shard_map/all_to_all | solution.py:30
  330.5 0.8 div.63
  (58 shorter events, 1.8 us)
Async XLA Ops:
  7.2 2.8 copy-start
  7.2 14.8 %copy-start.2 = (bf16[128,5120]{1,0:T(8,128)(2,1)S(1)}, bf16[128,5120]{1,0:T(8,128)(2,1)}, u32[]{:S(2)}) copy-start(bf16[128,5120]{1,0:T(8,128)(2,1)} %param.8) | copy-start | bytes 3932164
  7.2 126.4 %all-gather.2.cloned.1.call-start = ((), (), s32[]{:S(2)}) async-start(), calls=%async_computation.8 | async-start | bytes 13516800 | tf_op jit(solution)/shard_map/all_gather | solution.py:17
  10.8 19.9 %all-to-all-start = ((bf16[32,2,160]{2,1,0:T(2,128)(2,1)}), bf16[32,2,160]{2,1,0:T(2,128)(2,1)S(1)}, u32[]{:S(2)}, u32[]{:S(2)}) async-start(bf16[32,2,160]{2,1,0:T(2,128)(2,1)} %copy.51), calls=%async_computation | async-start | bytes 65536 | tf_op jit(solution)/shard_map/all_to_all | solution.py:146
  22.0 1.1 copy-start.11
  22.3 1.9 copy-start.12
  30.8 13.7 %all-to-all-start.3 = ((bf16[128,4,640]{0,2,1:T(8,128)(2,1)}), bf16[128,4,640]{0,2,1:T(8,128)(2,1)S(1)}, u32[]{:S(2)}, u32[]{:S(2)}) async-start(bf16[128,4,640]{0,2,1:T(8,128)(2,1)} %bitcast.18), calls=%async_computation.3 | async-start | bytes 1310720 | tf_op jit(solution)/shard_map/all_to_all | solution.py:170
  44.5 14.5 %all-to-all-start.2 = ((bf16[128,4,640]{0,2,1:T(8,128)(2,1)}), bf16[128,4,640]{0,2,1:T(8,128)(2,1)}, u32[]{:S(2)}, u32[]{:S(2)}) async-start(bf16[128,4,640]{0,2,1:T(8,128)(2,1)} %bitcast.16), calls=%async_computation.2 | async-start | bytes 1310720 | tf_op jit(solution)/shard_map/all_to_all | solution.py:171
  61.9 5.3 %copy-start.15 = (s32[3,512]{1,0:T(4,128)S(1)}, s32[3,512]{1,0:T(4,128)}, u32[]{:S(2)}) copy-start(s32[3,512]{1,0:T(4,128)} %param.9) | copy-start | bytes 18436
  61.9 91.7 %all-to-all-start.1 = ((bf16[4,128,5120]{2,1,0:T(8,128)(2,1)}), bf16[4,128,5120]{2,1,0:T(8,128)(2,1)}, u32[]{:S(2)}, u32[]{:S(2)}) async-start(bf16[4,128,5120]{2,1,0:T(8,128)(2,1)} %stack.2), calls=%async_computation.1 | async-start | bytes 10485760 | tf_op jit(solution)/shard_map/all_to_all | solution.py:158
  67.1 210.6 %reduce-scatter.3.cloned.1.call-start = ((), (), s32[]{:S(2)}) async-start(), calls=%async_computation.9 | async-start | bytes 7372800 | tf_op jit(solution)/shard_map/reduce_scatter | solution.py:24
  179.6 1.1 copy-start.4
  179.6 1.3 copy-start.5
  179.6 1.3 copy-start.7
  179.6 1.4 copy-start.8
  181.4 1.2 copy-start.13
  181.4 1.3 copy-start.14
  182.5 2.3 copy-start.3
  190.8 1.5 copy-start.6
  202.9 103.2 %copy-start.9 = (bf16[1,160,640]{2,1,0:T(8,128)(2,1)S(1)}, bf16[1,160,640]{2,1,0:T(8,128)(2,1)}, u32[]{:S(2)}) copy-start(bf16[1,160,640]{2,1,0:T(8,128)(2,1)} %param.12) | copy-start | bytes 614404
  202.9 103.2 %reduce-scatter.5.cloned.1.call-start = ((), (), s32[]{:S(2)}) async-start(), calls=%async_computation.10 | async-start | bytes 1024000 | tf_op jit(solution)/shard_map/reduce_scatter | solution.py:24
  307.1 15.8 %copy-start.10 = (bf16[160,640]{1,0:T(8,128)(2,1)S(1)}, bf16[160,640]{1,0:T(8,128)(2,1)}, u32[]{:S(2)}) copy-start(bf16[160,640]{1,0:T(8,128)(2,1)} %reduce-scatter.5.cloned.1.call-done) | copy-start | bytes 614404
  319.5 10.9 %all-to-all-start.4 = ((bf16[2,160,640]{2,1,0:T(8,128)(2,1)}), bf16[2,160,640]{2,1,0:T(8,128)(2,1)S(1)}, u32[]{:S(2)}, u32[]{:S(2)}) async-start(bf16[2,160,640]{2,1,0:T(8,128)(2,1)} %broadcast_in_dim.81), calls=%async_computation.6 | async-start | bytes 819200 | tf_op jit(solution)/shard_map/all_to_all | solution.py:30
  323.0 8.3 %copy-start.1 = (bf16[2,256,160]{1,2,0:T(8,128)(2,1)S(1)}, bf16[2,256,160]{1,2,0:T(8,128)(2,1)}, u32[]{:S(2)}) copy-start(bf16[2,256,160]{1,2,0:T(8,128)(2,1)} %param.11) | copy-start | bytes 491524
Sparse Core Ops, SparseCore 0:
  11.2 122.3 all-gather.1
  203.1 74.6 reduce-scatter.2
  280.3 25.7 reduce-scatter.4
